TPU v7x, 32 devices: a whole 2x2x4 slice. The times are simulated.
32 devices in a mesh: groups: 2 (over y), expert: 4 (over z), split: 2 (over x), pair: 2 (over core).
Axes of the slice: x: 2, y: 2, z: 4, core: 2. Of those that a mesh axis runs over, the one named last changes fastest.
Arguments:
- tokens: bfloat16 [64, 3584], P(('groups', 'expert'), ('split', 'pair')), parts along dimension 0, may hold values from -6 to 6
- routes: int32 [64, 2], P(('groups', 'expert')), parts along dimension 0, may hold values from 0 to 3, all different within a row; in each aligned block of 8 rows (0 to 7, 8 to 15, ...) at most 8 rows name the same one
- combine: float32 [64, 2], P(('groups', 'expert')), parts along dimension 0, may hold values from 0.05 to 1
- home: int32 [4], replicated, may hold values from 0 to 3, each once
- gate_up: bfloat16 [4, 3584, 2, 2560], P('expert', 'pair', None, 'split'), may hold values from -0.09375 to 0.09375
- down: bfloat16 [4, 2560, 3584], P('expert', ('split', 'pair')), may hold values from -0.15625 to 0.15625
Outputs:
- mixed: bfloat16 [64, 3584], P(('groups', 'expert'), ('split', 'pair')), parts along dimension 0
There are 2 independent parts, one for each index of `groups`. A program takes and returns all parts, laid end to end along the dimension named above; an argument that names none is the same for every part. Nothing has to cross between parts.
Inputs may be any that keep to these rules, and one draw needn't show every extreme that they name: `routes`: each row names 2 different experts. In the rows of one device no expert is named more than 8 times, and some expert reaches 8 in every draw. A permutation: expert e is held in storage slot home[e].
All inputs are finite; a program needn't handle non-finite values.
Results may differ from a plain program's by a relative error of at most 0.025.
Values may be sent and summed in bfloat16 or wider, within the bound.
A program may use at most 64 MiB of HBM per device.

v0:
```python
import jax
import jax.numpy as jnp
from jax import lax
from jax.sharding import PartitionSpec as P


def shards(tokens, routes, combine, home, gate_up, down):
    n_expert = lax.axis_size("expert")
    local_tokens = tokens.shape[0]
    chosen_count = routes.shape[1]
    experts_all = home.shape[0]
    experts_here = gate_up.shape[0]
    total_rows = experts_all * local_tokens
    width = gate_up.shape[1] * 2
    table_ids = jnp.arange(experts_all, dtype=jnp.int32)
    slot = jnp.sum(
        jnp.where(routes[:, :, None] == table_ids[None, None, :], home[None, None, :], 0), axis=-1
    )
    flat_slot = slot.reshape(-1)
    entries = flat_slot.shape[0]
    order_ids = jnp.arange(entries, dtype=jnp.int32)
    earlier = (flat_slot[:, None] == flat_slot[None, :]) & (order_ids[None, :] < order_ids[:, None])
    position = jnp.sum(earlier.astype(jnp.int32), axis=1)
    target = (flat_slot * local_tokens + position).reshape(local_tokens, chosen_count)
    row_ids = jnp.arange(total_rows, dtype=jnp.int32)
    hits = target[None, :, :] == row_ids[:, None, None]
    placing = jnp.sum(hits.astype(jnp.int32), axis=-1).astype(jnp.bfloat16)
    mixing = jnp.sum(jnp.where(hits, combine[None, :, :], jnp.float32(0.0)), axis=-1).T
    outgoing = jnp.dot(placing, tokens, preferred_element_type=jnp.float32).astype(jnp.bfloat16)
    arrived = lax.all_to_all(outgoing, "expert", split_axis=0, concat_axis=0, tiled=True)
    gathered = lax.all_gather(arrived, ("split", "pair"), axis=1, tiled=True)
    rows_each = n_expert * local_tokens
    inputs = gathered.reshape(n_expert, experts_here, local_tokens, width)
    inputs = jnp.swapaxes(inputs, 0, 1).reshape(experts_here, rows_each, width)
    pair_index = lax.axis_index("pair")
    half_width = gate_up.shape[1]
    own_half = lax.dynamic_slice_in_dim(inputs, pair_index * half_width, half_width, 2)
    before = jnp.einsum("erd,edgf->ergf", own_half, gate_up, preferred_element_type=jnp.float32)
    before = lax.psum_scatter(
        before.astype(jnp.bfloat16), "pair", scatter_dimension=3, tiled=True
    ).astype(jnp.float32)
    hidden = (jax.nn.silu(before[:, :, 0, :]) * before[:, :, 1, :]).astype(jnp.bfloat16)
    partial_value = jnp.einsum(
        "erf,efd->erd", hidden, down, preferred_element_type=jnp.float32
    ).astype(jnp.bfloat16)
    summed = (
        lax.psum_scatter(partial_value, ("split", "pair"), scatter_dimension=2, tiled=True)
        .astype(jnp.float32)
        .astype(jnp.bfloat16)
    )
    narrow = summed.shape[2]
    returning = jnp.swapaxes(summed.reshape(experts_here, n_expert, local_tokens, narrow), 0, 1)
    returning = returning.reshape(total_rows, narrow)
    results = lax.all_to_all(returning, "expert", split_axis=0, concat_axis=0, tiled=True)
    mixed = jnp.dot(mixing, results.astype(jnp.float32), precision=lax.Precision.HIGHEST)
    return mixed.astype(jnp.bfloat16)


def solution(mesh):
    placed = (
        P(("groups", "expert"), ("split", "pair")),
        P(("groups", "expert"), None),
        P(("groups", "expert"), None),
        P(),
        P("expert", "pair", None, "split"),
        P("expert", ("split", "pair"), None),
    )
    return jax.shard_map(
        shards,
        mesh=mesh,
        in_specs=placed,
        out_specs=P(("groups", "expert"), ("split", "pair")),
        check_vma=False,
    )
```

profile of v0, /device:TPU:0, one launch (start us, length us, event | category | flops | bytes accessed | tf_op | source)
XLA Modules:
  0.0 93.4 jit_solution(3916657868919815258)
XLA Ops:
  6.5 0.8 select_reduce_fusion.1
  7.3 0.1 copy.16
  7.4 0.1 eq.44
  7.5 0.2 convert_reduce_fusion.1
  7.7 0.1 reduce_sum.40
  7.8 0.1 copy.17
  7.9 0.1 convert_reduce_fusion
  7.9 0.0 copy-done
  7.9 0.8 fusion.16
  8.8 6.3 %all-to-all-start = ((bf16[4,8,896]{2,1,0:T(8,128)(2,1)}), bf16[4,8,896]{2,1,0:T(8,128)(2,1)S(1)}, u32[]{:S(2)}, u32[]{:S(2)}) async-start(bf16[4,8,896]{2,1,0:T(8,128)(2,1)} %fusion.16), calls=%async_computation | async-start | bytes 114688 | tf_op jit(solution)/shard_map/all_to_all | solution.py:30
  15.1 5.7 %all-to-all-done = bf16[4,8,896]{2,1,0:T(8,128)(2,1)S(1)} async-done(((bf16[4,8,896]{2,1,0:T(8,128)(2,1)}), bf16[4,8,896]{2,1,0:T(8,128)(2,1)S(1)}, u32[]{:S(2)}, u32[]{:S(2)}) %all-to-all-start) | async-done | bytes 57376 | tf_op jit(solution)/shard_map/all_to_all | solution.py:30
  20.8 5.7 %all_gather.3 = bf16[32,3584]{1,0:T(8,128)(2,1)S(1)} all-gather(bf16[32,896]{1,0:T(8,128)(2,1)S(1)} %bitcast.40), channel_id=1, replica_groups=mesh['groups'=2,'expert'=4,'split'=2,'pair'=2] {'split','pair'}, dimensions={1}, use_global_device_ids=true | all-gather | bytes 286720 | tf_op jit(solution)/shard_map/all_gather | solution.py:31
  26.5 5.3 %fusion.13 = bf16[1,32,2,1280]{3,1,2,0:T(8,128)(2,1)S(1)} fusion(bf16[1792,2,1280]{2,1,0:T(2,128)(2,1)} %bitcast.41, bf16[32,3584]{1,0:T(8,128)(2,1)S(1)} %all_gather.3, s32[]{:T(128)S(6)} %select_n.13), kind=kOutput, calls=%fused_computation.7 | convolution fusion | flops 293683200 | bytes 9453572 | tf_op jit(solution)/shard_map/erd,edgf->ergf/dot_general | solution.py:38
  31.8 0.0 copy-start.1
  31.8 0.5 copy.19
  32.3 1.0 %reshape.53 = bf16[1280,64]{1,0:T(8,128)(2,1)} reshape(bf16[1280,1,2,32]{3,2,1,0:T(2,128)(2,1)S(1)} %bitcast.38) | data formatting | bytes 327680
  33.4 0.0 reduce-scatter.7.cloned.1.call-update
  33.4 0.0 reduce-scatter.9.cloned.1.call-start
  33.4 6.4 %reduce-scatter.7.cloned.1.call-done = bf16[640,64]{1,0:T(8,128)(2,1)} async-done(((bf16[1280,64]{1,0:T(8,128)(2,1)}), bf16[640,64]{1,0:T(8,128)(2,1)}) %reduce-scatter.7.cloned.1.call-update) | async-done | bytes 81936
  39.8 1.1 %reshape.54 = bf16[640,1,2,32]{3,2,1,0:T(2,128)(2,1)S(1)} reshape(bf16[640,64]{1,0:T(8,128)(2,1)} %reduce-scatter.7.cloned.1.call-done) | data formatting | bytes 163840
  40.9 0.2 copy.20
  41.1 3.2 %fusion.7 = bf16[1,32,3584]{2,1,0:T(8,128)(2,1)S(1)} fusion(bf16[1,640,3584]{2,1,0:T(8,128)(2,1)} %param.11, f32[1,32,2,640]{3,1,2,0:T(8,128)S(1)} %convert_element_type.48), kind=kOutput, calls=%fused_computation.5 | convolution fusion | flops 147038208 | bytes 4980736 | tf_op jit(solution)/shard_map/erf,efd->erd/dot_general | solution.py:43
  44.3 2.4 %copy.21 = bf16[1,32,3584]{1,0,2:T(2,128)(2,1)S(1)} copy(bf16[1,32,3584]{2,1,0:T(8,128)(2,1)S(1)} %fusion.7) | data formatting | bytes 458752
  46.7 1.0 %copy.31 = bf16[3584,1,32]{2,0,1:T(8,128)(2,1)} copy(bf16[3584,1,32]{2,1,0:T(2,128)(2,1)S(1)} %bitcast.36) | data formatting | bytes 458752
  47.8 0.0 reduce-scatter.9.cloned.1.call-update
  47.8 25.3 %reduce-scatter.9.cloned.1.call-done = bf16[896,32]{1,0:T(8,128)(2,1)} async-done(((bf16[3584,32]{1,0:T(8,128)(2,1)}), bf16[896,32]{1,0:T(8,128)(2,1)}) %reduce-scatter.9.cloned.1.call-update) | async-done | bytes 57360
  73.1 1.2 %reshape_bitcast_fusion = bf16[1,32,896]{1,0,2:T(2,128)(2,1)S(1)} fusion(bf16[896,32]{1,0:T(8,128)(2,1)} %reduce-scatter.9.cloned.1.call-done), kind=kLoop, calls=%fused_computation.12 | loop fusion | bytes 114688
  74.3 1.2 %copy.22 = bf16[1,32,896]{2,1,0:T(8,128)(2,1)} copy(bf16[1,32,896]{1,0,2:T(2,128)(2,1)S(1)} %reshape_bitcast_fusion) | data formatting | bytes 114688
  75.5 4.6 %all-to-all-start.1 = ((bf16[4,8,896]{2,1,0:T(8,128)(2,1)}), bf16[4,8,896]{2,1,0:T(8,128)(2,1)S(1)}, u32[]{:S(2)}, u32[]{:S(2)}) async-start(bf16[4,8,896]{2,1,0:T(8,128)(2,1)} %bitcast.8), calls=%async_computation.1 | async-start | bytes 114688 | tf_op jit(solution)/shard_map/all_to_all | solution.py:54
  80.0 0.1 select_reduce_fusion
  80.1 5.6 %all-to-all-done.1 = bf16[4,8,896]{2,1,0:T(8,128)(2,1)S(1)} async-done(((bf16[4,8,896]{2,1,0:T(8,128)(2,1)}), bf16[4,8,896]{2,1,0:T(8,128)(2,1)S(1)}, u32[]{:S(2)}, u32[]{:S(2)}) %all-to-all-start.1) | async-done | bytes 57376 | tf_op jit(solution)/shard_map/all_to_all | solution.py:54
  85.8 0.7 convolution_convert_fusion.1
  (5 shorter events, 0.0 us)
Async XLA Ops:
  6.5 1.4 %copy-start = (bf16[8,896]{1,0:T(8,128)(2,1)S(1)}, bf16[8,896]{1,0:T(8,128)(2,1)}, u32[]{:S(2)}) copy-start(bf16[8,896]{1,0:T(8,128)(2,1)} %param.6) | copy-start | bytes 43012
  8.8 12.1 %all-to-all-start = ((bf16[4,8,896]{2,1,0:T(8,128)(2,1)}), bf16[4,8,896]{2,1,0:T(8,128)(2,1)S(1)}, u32[]{:S(2)}, u32[]{:S(2)}) async-start(bf16[4,8,896]{2,1,0:T(8,128)(2,1)} %fusion.16), calls=%async_computation | async-start | bytes 114688 | tf_op jit(solution)/shard_map/all_to_all | solution.py:30
  15.1 24.7 %reduce-scatter.7.cloned.1.call-start = ((), (), s32[]{:S(2)}) async-start(), calls=%async_computation.4 | async-start | bytes 491520
  31.8 48.3 %copy-start.1 = (f32[8,2]{0,1:T(2,128)S(1)}, f32[8,2]{0,1:T(2,128)}, u32[]{:S(2)}) copy-start(f32[8,2]{0,1:T(2,128)} %param.8) | copy-start | bytes 196
  33.4 39.7 %reduce-scatter.9.cloned.1.call-start = ((), (), s32[]{:S(2)}) async-start(), calls=%async_computation.5 | async-start | bytes 1146880
  75.5 10.3 %all-to-all-start.1 = ((bf16[4,8,896]{2,1,0:T(8,128)(2,1)}), bf16[4,8,896]{2,1,0:T(8,128)(2,1)S(1)}, u32[]{:S(2)}, u32[]{:S(2)}) async-start(bf16[4,8,896]{2,1,0:T(8,128)(2,1)} %bitcast.8), calls=%async_computation.1 | async-start | bytes 114688 | tf_op jit(solution)/shard_map/all_to_all | solution.py:54
Sparse Core Ops, SparseCore 0:
  33.5 6.2 reduce-scatter.6
  47.9 25.1 reduce-scatter.8
where the time goes:
time: 93.8 us; the launch traced here: 93.4 us
  waiting for transfers between devices  43.1 us (46%)
  between operations  13.5 us (14%)
  starting transfers between devices  11 us (12%)
  matrix products  10 us (11%)
  local copies, waits for them, and re-layouts  8.98 us (10%)
  blocking collectives  5.67 us (6%)
  other arithmetic  1.15 us (1%)
    unnamed x4, waiting for transfers between devices  31.7 us
    unnamed x12, local copies, waits for them, and re-layouts  8.65 us
    all_to_all x1, starting transfers between devices, shards(): lax.all_to_all(outgoing, 'expert', split_axis=0, concat_axis=0, tiled=True)  6.35 us
    all_to_all x1, waiting for transfers between devices, shards(): lax.all_to_all(outgoing, 'expert', split_axis=0, concat_axis=0, tiled=True)  5.72 us
    all_gather x1, blocking collectives, shards(): gathered = lax.all_gather(arrived, ('split', 'pair'), axis=1, tiled=True)  5.67 us
    all_to_all x1, waiting for transfers between devices, shards(): lax.all_to_all(returning, 'expert', split_axis=0, concat_axis=0, tiled=True)  5.65 us
    dot_general x1, matrix products, shards(): jnp.einsum('erd,edgf->ergf', own_half, gate_up, preferred_element_type=jn...  5.28 us
    all_to_all x1, starting transfers between devices, shards(): lax.all_to_all(returning, 'expert', split_axis=0, concat_axis=0, tiled=True)  4.59 us
  transfers between devices with their start and end apart: 4, of which 4 were waited for; matrix products, arithmetic and copies ran while one was open for 0% of the time, Pallas kernels for 0%

commit v1 on v0

--- a/solution.py
+++ b/solution.py
@@ -1,7 +1,259 @@
+import functools
 import jax
 import jax.numpy as jnp
 from jax import lax
+from jax.experimental import pallas as pl
+from jax.experimental.pallas import tpu as pltpu
 from jax.sharding import PartitionSpec as P
+
+MESH = pl.DeviceIdType.MESH
+LANES = 128
+
+
+def fused(
+    n_expert, chunks,
+    tokens_hbm, routes_ref, combine_ref, home_ref, gate_up_hbm, down_hbm, out_ref,
+    own, tok, spread, xi, wbuf, dbuf, mine, pre_out, pre_in, part_out, part_in, kept, stage, fin, mixbuf,
+    load_sem, w_sem, d_sem, tok_send, tok_recv, pre_send, pre_recv, part_send, part_recv, fin_send, fin_recv,
+):
+    groups, expert = lax.axis_index("groups"), lax.axis_index("expert")
+    split, pair = lax.axis_index("split"), lax.axis_index("pair")
+    partner = (groups, expert, split, 1 - pair)
+    rows, narrow = tokens_hbm.shape
+    depth = gate_up_hbm.shape[1]
+    half = gate_up_hbm.shape[3] // 2
+    blocks = half // LANES
+    all_rows = n_expert * rows
+
+    load = pltpu.make_async_copy(tokens_hbm, own, load_sem)
+    load.start()
+    step = depth // chunks
+    w_loads = []
+    for h in range(2):
+        at = pl.multiple_of(lax.rem(1 - pair + h, 2) * half, LANES)
+        for c in range(chunks):
+            w_loads.append(pltpu.make_async_copy(
+                gate_up_hbm.at[0, pl.ds(c * step, step), :, pl.ds(at, half)],
+                wbuf.at[h, pl.ds(c * step, step)], w_sem.at[h, c]))
+            w_loads[-1].start()
+    d_loads = []
+    for h in range(2):
+        core = lax.rem(1 - pair + h, 2)
+        for s in range(2):
+            at = pl.multiple_of((2 * s + core) * narrow, LANES)
+            d_loads.append(pltpu.make_async_copy(
+                down_hbm.at[0, :, pl.ds(at, narrow)],
+                dbuf.at[h, :, pl.ds(s * narrow, narrow)], d_sem.at[h, s]))
+            d_loads[-1].start()
+
+    barrier = pltpu.get_barrier_semaphore()
+    for de in range(n_expert):
+        for ds in range(2):
+            for dp in range(2):
+                if de + ds + dp:
+                    pl.semaphore_signal(barrier, inc=1, device_id=(
+                        groups, lax.rem(expert + de, n_expert), lax.rem(split + ds, 2), lax.rem(pair + dp, 2)),
+                        device_id_type=MESH)
+
+    experts_all = home_ref.shape[0]
+    chosen_count = routes_ref.shape[0]
+    square = (rows, rows)
+    diagonal = lax.broadcasted_iota(jnp.int32, square, 0) == lax.broadcasted_iota(jnp.int32, square, 1)
+    slot_rows = jnp.zeros((chosen_count, rows), jnp.int32)
+    for e in range(experts_all):
+        slot_rows = jnp.where(routes_ref[...] == e, home_ref[e], slot_rows)
+    for e in range(n_expert):
+        weight = jnp.sum(jnp.where(slot_rows == e, combine_ref[...], 0.0), axis=0, keepdims=True)
+        column = jnp.sum(jnp.where(diagonal, jnp.broadcast_to(weight, square), 0.0), axis=1, keepdims=True)
+        mixbuf[e] = jnp.broadcast_to(column, (rows, LANES))
+    shape = (LANES, 4 * LANES)
+    source = lax.broadcasted_iota(jnp.int32, shape, 0)
+    place = lax.broadcasted_iota(jnp.int32, shape, 1)
+    wanted = jnp.where(place < 2 * LANES, 2 * source, 2 * source + 2 * LANES + 1)
+    spread[...] = jnp.where(place == wanted, 1.0, 0.0).astype(jnp.bfloat16)
+
+    load.wait()
+    pl.semaphore_wait(barrier, 4 * n_expert - 1)
+
+    def tok_copy(de, ds):
+        return pltpu.make_async_remote_copy(
+            src_ref=own, dst_ref=tok.at[de, pair], send_sem=tok_send.at[de, ds], recv_sem=tok_recv.at[de, pair],
+            device_id=(groups, lax.rem(expert + de, n_expert), lax.rem(split + ds, 2), split), device_id_type=MESH)
+
+    local = pltpu.make_async_copy(own, tok.at[0, pair], tok_recv.at[0, pair])
+    order = sorted(range(n_expert), key=lambda de: -min(de, n_expert - de))
+    for de in order:
+        for ds in (1, 0):
+            if de or ds:
+                tok_copy(de, ds).start()
+
+    @pl.when(pair == split)
+    def _():
+        local.start()
+
+    @pl.when(pair != split)
+    def _():
+        tok_copy(0, 0).start()
+
+    for w_load in w_loads:
+        w_load.wait()
+    for de in range(n_expert):
+        for h in range(2):
+            pltpu.make_async_copy(own, tok.at[de, h], tok_recv.at[de, h]).wait()
+
+    pieces = []
+    for h in range(2):
+        whole = jnp.concatenate([tok[de, h].astype(jnp.float32) for de in range(n_expert)], axis=0)
+        for c in range(narrow // LANES):
+            pieces.append(whole[:, c * LANES:(c + 1) * LANES])
+    stacked = jnp.concatenate(pieces, axis=0).astype(jnp.bfloat16)
+    wide = jnp.dot(stacked, spread[...], preferred_element_type=jnp.float32).astype(jnp.bfloat16)
+    for c in range(len(pieces)):
+        at = c * 2 * LANES
+        xi[0:all_rows, at:at + 2 * LANES] = wide[c * all_rows:(c + 1) * all_rows, 0:2 * LANES]
+        xi[all_rows:, at:at + 2 * LANES] = wide[c * all_rows:(c + 1) * all_rows, 2 * LANES:]
+
+    def weights(number):
+        h, j = number // blocks, number % blocks
+        return wbuf[h, :, :, j * LANES:(j + 1) * LANES].reshape(2 * depth, LANES)
+
+    def pre_copy(k):
+        at = (0, 2 * (blocks // 2) * LANES, half)
+        cols = pl.ds(at[k], at[k + 1] - at[k])
+        return pltpu.make_async_remote_copy(
+            src_ref=pre_out.at[:, cols], dst_ref=pre_in.at[:, cols], send_sem=pre_send.at[k],
+            recv_sem=pre_recv.at[k], device_id=partner, device_id_type=MESH)
+
+    pre_copies = [pre_copy(0)] + ([pre_copy(1)] if blocks % 2 else [])
+    for n in range(blocks):
+        numbers = (2 * n, 2 * n + 1)
+        w = jnp.concatenate([weights(k) for k in numbers], axis=1)
+        value = jnp.dot(xi[...], w, preferred_element_type=jnp.float32)
+        for i, k in enumerate(numbers):
+            piece = value[:, i * LANES:(i + 1) * LANES]
+            if k < blocks:
+                pre_out[:, k * LANES:(k + 1) * LANES] = piece.astype(jnp.bfloat16)
+            else:
+                mine[:, (k - blocks) * LANES:(k - blocks + 1) * LANES] = piece
+        if n == blocks // 2 - 1:
+            pre_copies[0].start()
+        if blocks % 2 and n == blocks // 2:
+            pre_copies[1].start()
+
+    for copy in pre_copies:
+        copy.wait_recv()
+    total = mine[...] + pre_in[...].astype(jnp.float32)
+    gate, up = total[0:all_rows], total[all_rows:]
+    hidden = (gate / (1.0 + jnp.exp(-gate)) * up).astype(jnp.bfloat16)
+
+    for d_load in d_loads:
+        d_load.wait()
+    part_out[...] = jnp.dot(hidden, dbuf[0], preferred_element_type=jnp.float32).astype(jnp.bfloat16)
+    part = pltpu.make_async_remote_copy(
+        src_ref=part_out, dst_ref=part_in, send_sem=part_send, recv_sem=part_recv,
+        device_id=partner, device_id_type=MESH)
+    part.start()
+    kept[...] = jnp.dot(hidden, dbuf[1], preferred_element_type=jnp.float32)
+    part.wait_recv()
+
+    def fin_copy(de, ds):
+        return pltpu.make_async_remote_copy(
+            src_ref=stage.at[lax.rem(split + ds, 2), de], dst_ref=fin.at[de, ds],
+            send_sem=fin_send.at[de, ds], recv_sem=fin_recv.at[de, ds],
+            device_id=(groups, lax.rem(expert + de, n_expert), lax.rem(split + ds, 2), pair), device_id_type=MESH)
+
+    for de in order:
+        block = (n_expert - de) % n_expert
+        for s in range(2):
+            at = slice(s * narrow, (s + 1) * narrow)
+            lines = slice(block * rows, (block + 1) * rows)
+            stage[s, de] = (kept[lines, at] + part_in[:, at].astype(jnp.float32)[lines]).astype(jnp.bfloat16)
+        for ds in (1, 0):
+            if de or ds:
+                fin_copy(de, ds).start()
+
+    result = jnp.zeros((rows, narrow), jnp.float32)
+    for de in reversed(order):
+        source = lax.rem(expert + n_expert - de, n_expert)
+        pair_sum = jnp.zeros((rows, narrow), jnp.float32)
+        for ds in range(2):
+            if de or ds:
+                fin_copy(de, ds).wait_recv()
+                pair_sum += fin[de, ds].astype(jnp.float32)
+            else:
+                pair_sum += stage[split, 0].astype(jnp.float32)
+        result += mixbuf[source][:, 0:1] * pair_sum
+    out_ref[...] = result.astype(out_ref.dtype)
+
+    for de in range(n_expert):
+        for ds in range(2):
+            if de or ds:
+                tok_copy(de, ds).wait_send()
+                fin_copy(de, ds).wait_send()
+
+    @pl.when(pair != split)
+    def _():
+        tok_copy(0, 0).wait_send()
+
+    for copy in pre_copies:
+        copy.wait_send()
+    part.wait_send()
+
+
+def fused_shards(tokens, routes, combine, home, gate_up, down):
+    n_expert = lax.axis_size("expert")
+    rows, narrow = tokens.shape
+    depth, width = gate_up.shape[1], gate_up.shape[3]
+    half = width // 2
+    all_rows = n_expert * rows
+    bf16, f32 = jnp.bfloat16, jnp.float32
+    chunks = 4 if depth % 64 == 0 else 1
+    vmem, anywhere = pl.BlockSpec(memory_space=pltpu.VMEM), pl.BlockSpec(memory_space=pl.ANY)
+    dma = pltpu.SemaphoreType.DMA
+    return pl.pallas_call(
+        functools.partial(fused, n_expert, chunks),
+        out_shape=jax.ShapeDtypeStruct((rows, narrow), bf16),
+        in_specs=[anywhere, vmem, vmem, pl.BlockSpec(memory_space=pltpu.SMEM), anywhere, anywhere],
+        out_specs=vmem,
+        scratch_shapes=[
+            pltpu.VMEM((rows, narrow), bf16),
+            pltpu.VMEM((n_expert, 2, rows, narrow), bf16),
+            pltpu.VMEM((LANES, 4 * LANES), bf16),
+            pltpu.VMEM((2 * all_rows, 2 * depth), bf16),
+            pltpu.VMEM((2, depth, 2, half), bf16),
+            pltpu.VMEM((2, down.shape[1], 2 * narrow), bf16),
+            pltpu.VMEM((2 * all_rows, half), f32),
+            pltpu.VMEM((2 * all_rows, half), bf16),
+            pltpu.VMEM((2 * all_rows, half), bf16),
+            pltpu.VMEM((all_rows, 2 * narrow), bf16),
+            pltpu.VMEM((all_rows, 2 * narrow), bf16),
+            pltpu.VMEM((all_rows, 2 * narrow), f32),
+            pltpu.VMEM((2, n_expert, rows, narrow), bf16),
+            pltpu.VMEM((n_expert, 2, rows, narrow), bf16),
+            pltpu.VMEM((n_expert, rows, LANES), f32),
+            dma, dma((2, chunks)), dma((2, 2)),
+            dma((n_expert, 2)), dma((n_expert, 2)), dma((2,)), dma((2,)), dma, dma,
+            dma((n_expert, 2)), dma((n_expert, 2)),
+        ],
+        compiler_params=pltpu.CompilerParams(
+            collective_id=0, has_side_effects=True, vmem_limit_bytes=40 * 2**20),
+    )(tokens, routes.T, combine.T, home, gate_up, down)
+
+
+def fits(mesh):
+    return mesh.shape["split"] == 2 and mesh.shape["pair"] == 2
+
+
+def placed_body(mesh):
+    def body(tokens, routes, combine, home, gate_up, down):
+        aligned = (
+            tokens.shape[0] == 8 and tokens.shape[1] % LANES == 0 and gate_up.shape[0] == 1
+            and gate_up.shape[3] % (2 * LANES) == 0 and home.shape[0] == mesh.shape["expert"]
+        )
+        chosen = fused_shards if fits(mesh) and aligned else shards
+        return chosen(tokens, routes, combine, home, gate_up, down)
+
+    return body
 
 
 def shards(tokens, routes, combine, home, gate_up, down):
@@ -66,7 +318,7 @@
         P("expert", ("split", "pair"), None),
     )
     return jax.shard_map(
-        shards,
+        placed_body(mesh),
         mesh=mesh,
         in_specs=placed,
         out_specs=P(("groups", "expert"), ("split", "pair")),

time: 93.8 us -> 33.5 us (0.36)
  waiting for transfers between devices: 43.1 us -> 0 us
  Pallas kernels: 0 us -> 24 us
  between operations: 13.5 us -> 0.02 us
  starting transfers between devices: 11 us -> 0 us
  matrix products: 10 us -> 0 us
  blocking collectives: 5.67 us -> 0 us
  other arithmetic: 1.15 us -> 0 us
    unnamed x4 -> x0, waiting for transfers between devices: 31.7 us -> none
    pallas_call x0 -> x1, Pallas kernels: none -> 24 us  [fused_shards(): pl.pallas_call(functools.partial(fused, n_expert, chunks), out_shape=jax....]
    all_to_all x2 -> x0, waiting for transfers between devices: 11.4 us -> none  [the longest x1 5.72 us: shards(): lax.all_to_all(outgoing, 'expert', split_axis=0, concat_axis=0, tiled=True)]
    all_to_all x2 -> x0, starting transfers between devices: 10.9 us -> none  [the longest x1 6.35 us: shards(): lax.all_to_all(outgoing, 'expert', split_axis=0, concat_axis=0, tiled=True)]
    dot_general x4 -> x0, matrix products: 10 us -> none  [the longest x1 5.28 us: shards(): jnp.einsum('erd,edgf->ergf', own_half, gate_up, preferred_element_type=jn...]
    all_gather x1 -> x0, blocking collectives: 5.67 us -> none  [shards(): gathered = lax.all_gather(arrived, ('split', 'pair'), axis=1, tiled=True)]
    reduce_sum x4 -> x0, other arithmetic: 1.13 us -> none  [the longest x1 0.79 us: shards(): jnp.sum(jnp.where(routes[:, :, None] == table_ids[None, None, :], home[No...]
    unnamed x12 -> x13, local copies, waits for them, and re-layouts: 8.65 us -> 9.23 us
  transfers between devices with their start and end apart: 4 -> 0, of which waited for: 4 -> 0; matrix products, arithmetic and copies ran while one was open for 0% -> 0% of each run, Pallas kernels for 0% -> 0%
where the time goes in v1:
time: 33.5 us; the launch traced here: 33.2 us
  Pallas kernels  24 us (72%)
  local copies, waits for them, and re-layouts  9.23 us (28%)
    pallas_call x1, Pallas kernels, fused_shards(): pl.pallas_call(functools.partial(fused, n_expert, chunks), out_shape=jax....  24 us
    unnamed x13, local copies, waits for them, and re-layouts  9.23 us

profile of v1, /device:TPU:0, one launch (start us, length us, event | category | flops | bytes accessed | tf_op | source)
XLA Modules:
  0.0 33.2 jit_solution(18098933338077666300)
XLA Ops:
  0.0 0.0 copy-start
  0.0 3.6 %copy-done = bf16[1,1792,2,1280]{3,2,1,0:T(2,128)(2,1)S(1)} copy-done((bf16[1,1792,2,1280]{3,2,1,0:T(2,128)(2,1)S(1)}, bf16[1,1792,2,1280]{3,2,1,0:T(2,128)(2,1)}, u32[]{:S(2)}) %copy-start) | copy-done | bytes 9175064
  3.6 0.0 copy-start.1
  3.6 2.3 %copy-done.1 = bf16[1,640,3584]{2,1,0:T(8,128)(2,1)S(1)} copy-done((bf16[1,640,3584]{2,1,0:T(8,128)(2,1)S(1)}, bf16[1,640,3584]{2,1,0:T(8,128)(2,1)}, u32[]{:S(2)}) %copy-start.1) | copy-done | bytes 4587544
  5.9 0.0 copy-start.2
  5.9 0.7 %copy-done.2 = bf16[8,896]{1,0:T(8,128)(2,1)S(1)} copy-done((bf16[8,896]{1,0:T(8,128)(2,1)S(1)}, bf16[8,896]{1,0:T(8,128)(2,1)}, u32[]{:S(2)}) %copy-start.2) | copy-done | bytes 14360
  6.6 0.0 copy-start.3
  6.6 0.7 %copy-done.3 = s32[8,2]{0,1:T(2,128)S(1)} copy-done((s32[8,2]{0,1:T(2,128)S(1)}, s32[8,2]{0,1:T(2,128)}, u32[]{:S(2)}) %copy-start.3) | copy-done | bytes 88
  7.3 0.0 copy-start.4
  7.3 0.7 %copy-done.4 = f32[8,2]{0,1:T(2,128)S(1)} copy-done((f32[8,2]{0,1:T(2,128)S(1)}, f32[8,2]{0,1:T(2,128)}, u32[]{:S(2)}) %copy-start.4) | copy-done | bytes 88
  8.0 0.0 copy-start.5
  8.0 0.7 %copy-done.5 = s32[4]{0:T(128)S(1)} copy-done((s32[4]{0:T(128)S(1)}, s32[4]{0:T(128)}, u32[]{:S(2)}) %copy-start.5) | copy-done | bytes 40
  8.6 24.0 %shard_map.64 = bf16[8,896]{1,0:T(8,128)(2,1)S(1)} custom-call(bf16[8,896]{1,0:T(8,128)(2,1)S(1)} %copy-done.2, s32[2,8]{1,0:T(2,128)S(1)} %bitcast.2, f32[2,8]{1,0:T(2,128)S(1)} %bitcast.3, s32[4]{0:T(128)S(1)} %copy-done.5, bf16[1,1792,2,1280]{3,2,1,0:T(2,128)(2,1)S(1)} %copy-done, bf16[1,640,3584]{2,1,0:T(8,128)(2,1)S(1)} %copy-done.1), custom_call_target="tpu_custom_call" | custom-call | tf_op jit(solution)/shard_map/pallas_call | solution.py:213
  32.6 0.6 %copy.8 = bf16[8,896]{1,0:T(8,128)(2,1)} copy(bf16[8,896]{1,0:T(8,128)(2,1)S(1)} %shard_map.64) | data formatting | bytes 28672
Async XLA Ops:
  0.0 3.6 %copy-start = (bf16[1,1792,2,1280]{3,2,1,0:T(2,128)(2,1)S(1)}, bf16[1,1792,2,1280]{3,2,1,0:T(2,128)(2,1)}, u32[]{:S(2)}) copy-start(bf16[1,1792,2,1280]{3,2,1,0:T(2,128)(2,1)} %gate_up_hbm.1) | copy-start | bytes 27525124
  3.6 2.3 %copy-start.1 = (bf16[1,640,3584]{2,1,0:T(8,128)(2,1)S(1)}, bf16[1,640,3584]{2,1,0:T(8,128)(2,1)}, u32[]{:S(2)}) copy-start(bf16[1,640,3584]{2,1,0:T(8,128)(2,1)} %down_hbm.1) | copy-start | bytes 13762564
  5.9 0.7 %copy-start.2 = (bf16[8,896]{1,0:T(8,128)(2,1)S(1)}, bf16[8,896]{1,0:T(8,128)(2,1)}, u32[]{:S(2)}) copy-start(bf16[8,896]{1,0:T(8,128)(2,1)} %tokens_hbm.1) | copy-start | bytes 43012
  6.6 0.7 %copy-start.3 = (s32[8,2]{0,1:T(2,128)S(1)}, s32[8,2]{0,1:T(2,128)}, u32[]{:S(2)}) copy-start(s32[8,2]{0,1:T(2,128)} %param.7) | copy-start | bytes 196
  7.3 0.7 %copy-start.4 = (f32[8,2]{0,1:T(2,128)S(1)}, f32[8,2]{0,1:T(2,128)}, u32[]{:S(2)}) copy-start(f32[8,2]{0,1:T(2,128)} %param.8) | copy-start | bytes 196
  8.0 0.7 %copy-start.5 = (s32[4]{0:T(128)S(1)}, s32[4]{0:T(128)}, u32[]{:S(2)}) copy-start(s32[4]{0:T(128)} %home_ref.1) | copy-start | bytes 52

commit v2 on v1

--- a/solution.py
+++ b/solution.py
@@ -12,8 +12,8 @@
 
 def fused(
     n_expert, chunks,
-    tokens_hbm, routes_ref, combine_ref, home_ref, gate_up_hbm, down_hbm, out_ref,
-    own, tok, spread, xi, wbuf, dbuf, mine, pre_out, pre_in, part_out, part_in, kept, stage, fin, mixbuf,
+    tokens_hbm, routes_hbm, combine_hbm, home_hbm, gate_up_hbm, down_hbm, out_ref,
+    routes_ref, combine_ref, home_ref, own, tok, spread, xi, wbuf, dbuf, mine, pre_out, pre_in, part_out, part_in, kept, stage, fin, mixbuf,
     load_sem, w_sem, d_sem, tok_send, tok_recv, pre_send, pre_recv, part_send, part_recv, fin_send, fin_recv,
 ):
     groups, expert = lax.axis_index("groups"), lax.axis_index("expert")
@@ -25,8 +25,15 @@
     blocks = half // LANES
     all_rows = n_expert * rows
 
-    load = pltpu.make_async_copy(tokens_hbm, own, load_sem)
+    load = pltpu.make_async_copy(tokens_hbm, own, load_sem.at[0])
     load.start()
+    tables = [
+        pltpu.make_async_copy(routes_hbm, routes_ref, load_sem.at[1]),
+        pltpu.make_async_copy(combine_hbm, combine_ref, load_sem.at[2]),
+        pltpu.make_async_copy(home_hbm, home_ref, load_sem.at[3]),
+    ]
+    for table in tables:
+        table.start()
     step = depth // chunks
     w_loads = []
     for h in range(2):
@@ -55,6 +62,31 @@
                         groups, lax.rem(expert + de, n_expert), lax.rem(split + ds, 2), lax.rem(pair + dp, 2)),
                         device_id_type=MESH)
 
+    load.wait()
+    pl.semaphore_wait(barrier, 4 * n_expert - 1)
+
+    def tok_copy(de, ds):
+        return pltpu.make_async_remote_copy(
+            src_ref=own, dst_ref=tok.at[de, pair], send_sem=tok_send.at[de, ds], recv_sem=tok_recv.at[de, pair],
+            device_id=(groups, lax.rem(expert + de, n_expert), lax.rem(split + ds, 2), split), device_id_type=MESH)
+
+    local = pltpu.make_async_copy(own, tok.at[0, pair], tok_recv.at[0, pair])
+    order = sorted(range(n_expert), key=lambda de: -min(de, n_expert - de))
+    for de in order:
+        for ds in (1, 0):
+            if de or ds:
+                tok_copy(de, ds).start()
+
+    @pl.when(pair == split)
+    def _():
+        local.start()
+
+    @pl.when(pair != split)
+    def _():
+        tok_copy(0, 0).start()
+
+    for table in tables:
+        table.wait()
     experts_all = home_ref.shape[0]
     chosen_count = routes_ref.shape[0]
     square = (rows, rows)
@@ -72,29 +104,6 @@
     wanted = jnp.where(place < 2 * LANES, 2 * source, 2 * source + 2 * LANES + 1)
     spread[...] = jnp.where(place == wanted, 1.0, 0.0).astype(jnp.bfloat16)
 
-    load.wait()
-    pl.semaphore_wait(barrier, 4 * n_expert - 1)
-
-    def tok_copy(de, ds):
-        return pltpu.make_async_remote_copy(
-            src_ref=own, dst_ref=tok.at[de, pair], send_sem=tok_send.at[de, ds], recv_sem=tok_recv.at[de, pair],
-            device_id=(groups, lax.rem(expert + de, n_expert), lax.rem(split + ds, 2), split), device_id_type=MESH)
-
-    local = pltpu.make_async_copy(own, tok.at[0, pair], tok_recv.at[0, pair])
-    order = sorted(range(n_expert), key=lambda de: -min(de, n_expert - de))
-    for de in order:
-        for ds in (1, 0):
-            if de or ds:
-                tok_copy(de, ds).start()
-
-    @pl.when(pair == split)
-    def _():
-        local.start()
-
-    @pl.when(pair != split)
-    def _():
-        tok_copy(0, 0).start()
-
     for w_load in w_loads:
         w_load.wait()
     for de in range(n_expert):
@@ -208,14 +217,17 @@
     all_rows = n_expert * rows
     bf16, f32 = jnp.bfloat16, jnp.float32
     chunks = 4 if depth % 64 == 0 else 1
-    vmem, anywhere = pl.BlockSpec(memory_space=pltpu.VMEM), pl.BlockSpec(memory_space=pl.ANY)
+    in_hbm = pl.BlockSpec(memory_space=pltpu.HBM)
     dma = pltpu.SemaphoreType.DMA
     return pl.pallas_call(
         functools.partial(fused, n_expert, chunks),
         out_shape=jax.ShapeDtypeStruct((rows, narrow), bf16),
-        in_specs=[anywhere, vmem, vmem, pl.BlockSpec(memory_space=pltpu.SMEM), anywhere, anywhere],
-        out_specs=vmem,
+        in_specs=[in_hbm] * 6,
+        out_specs=pl.BlockSpec(memory_space=pltpu.VMEM),
         scratch_shapes=[
+            pltpu.VMEM(routes.shape[::-1], jnp.int32),
+            pltpu.VMEM(combine.shape[::-1], f32),
+            pltpu.SMEM(home.shape, jnp.int32),
             pltpu.VMEM((rows, narrow), bf16),
             pltpu.VMEM((n_expert, 2, rows, narrow), bf16),
             pltpu.VMEM((LANES, 4 * LANES), bf16),
@@ -231,12 +243,12 @@
             pltpu.VMEM((2, n_expert, rows, narrow), bf16),
             pltpu.VMEM((n_expert, 2, rows, narrow), bf16),
             pltpu.VMEM((n_expert, rows, LANES), f32),
-            dma, dma((2, chunks)), dma((2, 2)),
+            dma((4,)), dma((2, chunks)), dma((2, 2)),
             dma((n_expert, 2)), dma((n_expert, 2)), dma((2,)), dma((2,)), dma, dma,
             dma((n_expert, 2)), dma((n_expert, 2)),
         ],
         compiler_params=pltpu.CompilerParams(
-            collective_id=0, has_side_effects=True, vmem_limit_bytes=40 * 2**20),
+            collective_id=0, has_side_effects=True, vmem_limit_bytes=67_043_328),
     )(tokens, routes.T, combine.T, home, gate_up, down)
 
 

time: 33.5 us -> 23.9 us (0.71)
  local copies, waits for them, and re-layouts: 9.23 us -> 1.31 us
  Pallas kernels: 24 us -> 22.4 us
    unnamed x13 -> x1, local copies, waits for them, and re-layouts: 9.23 us -> 1.31 us
    pallas_call x1, Pallas kernels: 24 us -> 22.4 us  [fused_shards(): pl.pallas_call(functools.partial(fused, n_expert, chunks), out_shape=jax....]
where the time goes in v2:
time: 23.9 us; the launch traced here: 23.7 us
  Pallas kernels  22.4 us (94%)
  local copies, waits for them, and re-layouts  1.31 us (5%)
    pallas_call x1, Pallas kernels, fused_shards(): pl.pallas_call(functools.partial(fused, n_expert, chunks), out_shape=jax....  22.4 us
    unnamed x1, local copies, waits for them, and re-layouts  1.31 us

profile of v2, /device:TPU:0, one launch (start us, length us, event | category | flops | bytes accessed | tf_op | source)
XLA Modules:
  0.0 23.7 jit_solution(503630292965992289)
XLA Ops:
  0.0 22.4 %shard_map.64 = bf16[8,896]{1,0:T(8,128)(2,1)} custom-call(bf16[8,896]{1,0:T(8,128)(2,1)} %tokens_hbm.1, s32[2,8]{1,0:T(2,128)} %bitcast.2, f32[2,8]{1,0:T(2,128)} %bitcast.3, s32[4]{0:T(128)} %home_hbm.1, bf16[1,1792,2,1280]{3,2,1,0:T(2,128)(2,1)} %gate_up_hbm.1, bf16[1,640,3584]{2,1,0:T(8,128)(2,1)} %down_hbm.1), custom_call_target="tpu_custom_call" | custom-call | tf_op jit(solution)/shard_map/pallas_call | solution.py:222
  22.4 1.3 %copy.8 = bf16[8,896]{1,0:T(8,128)(2,1)} copy(bf16[8,896]{1,0:T(8,128)(2,1)} %shard_map.64) | data formatting | bytes 28672

commit v3 on v2

--- a/solution.py
+++ b/solution.py
@@ -248,8 +248,9 @@
             dma((n_expert, 2)), dma((n_expert, 2)),
         ],
         compiler_params=pltpu.CompilerParams(
-            collective_id=0, has_side_effects=True, vmem_limit_bytes=67_043_328),
-    )(tokens, routes.T, combine.T, home, gate_up, down)
+            collective_id=0, has_side_effects=True, vmem_limit_bytes=40 * 2**20),
+    )(*[pltpu.with_memory_space_constraint(x, pltpu.HBM)
+        for x in (tokens, routes.T, combine.T, home, gate_up, down)])
 
 
 def fits(mesh):

time: 23.9 us -> 22.5 us (0.941)
  local copies, waits for them, and re-layouts: 1.31 us -> 0.6 us
  Pallas kernels: 22.4 us -> 21.8 us
    unnamed x1, local copies, waits for them, and re-layouts: 1.31 us -> 0.6 us
    pallas_call x1, Pallas kernels: 22.4 us -> 21.8 us  [fused_shards(): pl.pallas_call(functools.partial(fused, n_expert, chunks), out_shape=jax....]
where the time goes in v3:
time: 22.5 us; the launch traced here: 22.4 us
  Pallas kernels  21.8 us (97%)
  local copies, waits for them, and re-layouts  0.6 us (3%)
    pallas_call x1, Pallas kernels, fused_shards(): pl.pallas_call(functools.partial(fused, n_expert, chunks), out_shape=jax....  21.8 us
    unnamed x1, local copies, waits for them, and re-layouts  0.6 us

profile of v3, /device:TPU:0, one launch (start us, length us, event | category | flops | bytes accessed | tf_op | source)
XLA Modules:
  0.0 22.4 jit_solution(213036021645236545)
XLA Ops:
  0.0 21.8 %shard_map.64 = bf16[8,896]{1,0:T(8,128)(2,1)S(1)} custom-call(bf16[8,896]{1,0:T(8,128)(2,1)} %tokens_hbm.1, s32[2,8]{1,0:T(2,128)} %bitcast.2, f32[2,8]{1,0:T(2,128)} %bitcast.3, s32[4]{0:T(128)} %home_hbm.1, bf16[1,1792,2,1280]{3,2,1,0:T(2,128)(2,1)} %gate_up_hbm.1, bf16[1,640,3584]{2,1,0:T(8,128)(2,1)} %down_hbm.1), custom_call_target="tpu_custom_call" | custom-call | tf_op jit(solution)/shard_map/pallas_call | solution.py:222
  21.8 0.6 %copy.8 = bf16[8,896]{1,0:T(8,128)(2,1)} copy(bf16[8,896]{1,0:T(8,128)(2,1)S(1)} %shard_map.64) | data formatting | bytes 28672
